TPU v7x, 256 devices: a 2x2x32 block of a 4x8x32 slice. The times are simulated.
256 devices in a mesh: cohort: 4 (over x, y), tile: 64 (over z, core).
Axes of the slice: x: 2, y: 2, z: 32, core: 2. Of those that a mesh axis runs over, the one named last changes fastest.
The devices are a block of a 4x8x32 slice.
Arguments:
- dosage: bfloat16 [4096, 8192], P(('cohort', 'tile')), parts along dimension 0, may hold values from 0 to 2
- covars: float32 [4096, 16], P(('cohort', 'tile')), parts along dimension 0, may hold values from -12 to 12, as said below
- phenotypes: float32 [4096, 7168], P(('cohort', 'tile')), parts along dimension 0, may hold values from -100 to 100
Outputs:
- mean_chi: float32 [28672], P(('cohort', 'tile')), parts along dimension 0
- hit_rate: float32 [28672], P(('cohort', 'tile')), parts along dimension 0
There are 4 independent parts, one for each index of `cohort`. A program takes and returns all parts, laid end to end along the dimension named above; each array names one. Nothing has to cross between parts.
Inputs may be any that keep to these rules, and one draw needn't show every extreme that they name: `covars`: each covariate column has its own mean and spread.
All inputs are finite; a program needn't handle non-finite values.
Results may differ from a plain program's by a relative error of at most 0.003.
Values may be sent and summed in bfloat16 or wider, within the bound.
A program may use at most 64 MiB of HBM per device.

v0:
```python
import jax
import jax.numpy as jnp
from jax import lax
from jax.sharding import Mesh
from jax.sharding import PartitionSpec as P

TILE = ("tile_0", "tile_1")
COHORT_TILE = ("cohort", "tile_0", "tile_1")


def in_order(parts, dim):
    shape = list(parts.shape[1:])
    shape[dim] *= parts.shape[0]
    return jnp.moveaxis(parts, 0, dim).reshape(shape)


def gather_in_order(shard, axes, turns):
    parts = shard
    for k in turns:
        parts = lax.all_gather(parts, axes[k])
    done = turns[::-1]
    back = [done.index(k) for k in range(len(axes))]
    parts = parts.transpose(*back, *range(len(axes), parts.ndim))
    return parts.reshape(-1, *shard.shape)


def whole_of(shard, axes, turns, dim):
    return in_order(gather_in_order(shard, axes, turns), dim)


def local(dosage, covars, phenotypes):
    highest = lax.Precision.HIGHEST
    devices = lax.axis_size(TILE)
    local_rows = dosage.shape[0]
    variants = dosage.shape[1]
    samples = local_rows * devices
    genes_all = phenotypes.shape[1]
    gene_own = genes_all // devices
    scale_root = jnp.sqrt(jnp.float32(samples))
    covars_all = whole_of(covars, TILE, (0, 1), 0)
    dose_all = lax.all_gather(dosage, TILE, axis=0, tiled=True)
    pheno_own = lax.all_to_all(phenotypes, TILE, split_axis=1, concat_axis=0, tiled=True)
    gram = jnp.dot(covars_all.T, covars_all, precision=highest, preferred_element_type=jnp.float32)
    factor = jnp.linalg.cholesky(gram)
    cov_pheno = jnp.dot(
        covars_all.T, pheno_own, precision=highest, preferred_element_type=jnp.float32
    )
    beta_pheno = jax.scipy.linalg.cho_solve((factor, True), cov_pheno)
    pheno_resid = pheno_own - jnp.dot(
        covars_all, beta_pheno, precision=highest, preferred_element_type=jnp.float32
    )
    pheno_sumsq = jnp.sum(pheno_resid * pheno_resid, axis=0)
    pheno_bf = pheno_resid.astype(jnp.bfloat16)
    pheno_var = pheno_sumsq / samples + 0.1
    width = 1024
    blocks = variants // width

    def one_block(index, totals):
        start = index * width
        dose_block = lax.dynamic_slice_in_dim(dose_all, start, width, 1).astype(jnp.float32)
        cov_dose = jnp.dot(
            covars_all.T, dose_block, precision=highest, preferred_element_type=jnp.float32
        )
        beta_dose = jax.scipy.linalg.cho_solve((factor, True), cov_dose)
        dose_resid = dose_block - jnp.dot(
            covars_all, beta_dose, precision=highest, preferred_element_type=jnp.float32
        )
        dose_var = jnp.sum(dose_resid * dose_resid, axis=0) / samples + 0.1
        cross = lax.dot_general(
            pheno_bf,
            dose_resid.astype(jnp.bfloat16),
            (((0,), (0,)), ((), ())),
            preferred_element_type=jnp.float32,
        )
        zscore = cross / (scale_root * jnp.sqrt(pheno_var[:, None] * dose_var[None, :]))
        chi_square = zscore * zscore
        return (
            totals[0] + jnp.sum(chi_square, axis=1),
            totals[1] + jnp.sum(jax.nn.sigmoid(2.0 * (chi_square - 4.0)), axis=1),
        )

    zeros = jnp.zeros((gene_own,), jnp.float32)
    chi_total, hit_total = lax.fori_loop(0, blocks, one_block, (zeros, zeros))
    return (chi_total / variants, 20.0 / variants * hit_total)


def solution(mesh):
    finer = Mesh(mesh.devices.reshape(mesh.shape["cohort"], 32, 2), ("cohort", "tile_0", "tile_1"))
    return jax.shard_map(
        local,
        mesh=finer,
        in_specs=(P(COHORT_TILE, None), P(COHORT_TILE, None), P(COHORT_TILE, None)),
        out_specs=(P(COHORT_TILE), P(COHORT_TILE)),
        check_vma=False,
    )
```

profile of v0, /device:TPU:37, one launch (start us, length us, event | category | flops | bytes accessed | tf_op | source)
XLA Modules:
  0.0 319.9 jit_solution(15411580369733609212)
XLA Ops:
  8.0 1.3 all_to_all.14
  10.4 34.3 %all-to-all-start = ((f32[16,64,112]{2,0,1:T(8,128)}), f32[16,64,112]{2,0,1:T(8,128)S(1)}, u32[]{:S(2)}, u32[]{:S(2)}) async-start(f32[16,64,112]{2,0,1:T(8,128)} %copy.19), calls=%async_computation | async-start | bytes 1048576 | tf_op jit(solution)/shard_map/all_to_all | solution.py:42
  44.8 96.4 %all-gather = f32[512,16]{1,0:T(8,128)S(1)} all-gather(f32[16,16]{1,0:T(8,128)} %param.6), channel_id=2, replica_groups=mesh['cohort'=4,'tile_0'=32,'tile_1'=2] {'tile_0'}, dimensions={0}, use_global_device_ids=true | all-gather | bytes 33792 | tf_op jit(solution)/shard_map/all_gather | solution.py:20
  141.2 9.8 %all-gather.1 = f32[64,16,16]{2,1,0:T(8,128)S(1)} all-gather(f32[32,16,16]{2,1,0:T(8,128)S(1)} %bitcast.97), channel_id=3, replica_groups=mesh['cohort'=4,'tile_0'=32,'tile_1'=2] {'tile_1'}, dimensions={0}, use_global_device_ids=true | all-gather | bytes 98304 | tf_op jit(solution)/shard_map/all_gather | solution.py:20
  151.8 1.5 cholesky.18
  154.6 1.2 custom-call.24
  159.2 55.1 %all-gather.4.cloned.1.call-done = bf16[1024,8192]{1,0:T(8,128)(2,1)} async-done(((bf16[16,8192]{1,0:T(8,128)(2,1)}), bf16[1024,8192]{1,0:T(8,128)(2,1)}) %all-gather.4.cloned.1.call-update) | async-done | bytes 16777232 | tf_op jit(solution)/shard_map/all_gather | solution.py:41
  214.3 98.2 %while.18 = (s32[]{:T(128)}, f32[112]{0:T(128)S(1)}, f32[112]{0:T(128)S(1)}, bf16[1024,8192]{1,0:T(8,128)(2,1)}, f32[16,16]{1,0:T(8,128)S(1)}, /*index=5*/f32[10...) while((s32[]{:T(128)}, f32[112]{0:T(128)S(1)}, ...), condition=%wide.region_7.8_spmd.clone, body=%wide.region_3.7_spmd.clone.sunk | while | flops 652428992 | bytes 15458425 | solution.py:83
  214.3 2.5 fusion.67
  218.5 5.4 %multiply_reduce_fusion.3 = (f32[1024]{0:T(1024)S(1)}, f32[1024,1024]{0,1:T(8,128)S(1)}) fusion(bf16[1024,8192]{1,0:T(8,128)(2,1)} %get-tuple-element.371, s32[]{:T(128)S(6)} %select_n.19, f32[16,1024]{1,0:T(8,128)S(1)} %fusion.69, f32[1024,16]{0,1:T(8,128)S(1)} %get-tuple-element.373), kind=kOutput, calls=%fused_computation.1.clone.1 | convolution fusion | flops 205519872 | bytes 6426628 | tf_op jit(solution)/shard_map/while/body/eval_jaxpr/dot_general | solution.py:65
  223.9 2.6 fusion.70
  226.5 2.5 fusion.67
  230.8 5.4 %multiply_reduce_fusion.3 = (f32[1024]{0:T(1024)S(1)}, f32[1024,1024]{0,1:T(8,128)S(1)}) fusion(bf16[1024,8192]{1,0:T(8,128)(2,1)} %get-tuple-element.371, s32[]{:T(128)S(6)} %select_n.19, f32[16,1024]{1,0:T(8,128)S(1)} %fusion.69, f32[1024,16]{0,1:T(8,128)S(1)} %get-tuple-element.373), kind=kOutput, calls=%fused_computation.1.clone.1 | convolution fusion | flops 205519872 | bytes 6426628 | tf_op jit(solution)/shard_map/while/body/eval_jaxpr/dot_general | solution.py:65
  236.2 2.6 fusion.70
  238.8 2.5 fusion.67
  243.1 5.4 %multiply_reduce_fusion.3 = (f32[1024]{0:T(1024)S(1)}, f32[1024,1024]{0,1:T(8,128)S(1)}) fusion(bf16[1024,8192]{1,0:T(8,128)(2,1)} %get-tuple-element.371, s32[]{:T(128)S(6)} %select_n.19, f32[16,1024]{1,0:T(8,128)S(1)} %fusion.69, f32[1024,16]{0,1:T(8,128)S(1)} %get-tuple-element.373), kind=kOutput, calls=%fused_computation.1.clone.1 | convolution fusion | flops 205519872 | bytes 6426628 | tf_op jit(solution)/shard_map/while/body/eval_jaxpr/dot_general | solution.py:65
  248.5 2.6 fusion.70
  251.1 2.5 fusion.67
  255.3 5.4 %multiply_reduce_fusion.3 = (f32[1024]{0:T(1024)S(1)}, f32[1024,1024]{0,1:T(8,128)S(1)}) fusion(bf16[1024,8192]{1,0:T(8,128)(2,1)} %get-tuple-element.371, s32[]{:T(128)S(6)} %select_n.19, f32[16,1024]{1,0:T(8,128)S(1)} %fusion.69, f32[1024,16]{0,1:T(8,128)S(1)} %get-tuple-element.373), kind=kOutput, calls=%fused_computation.1.clone.1 | convolution fusion | flops 205519872 | bytes 6426628 | tf_op jit(solution)/shard_map/while/body/eval_jaxpr/dot_general | solution.py:65
  260.8 2.6 fusion.70
  263.4 2.5 fusion.67
  267.6 5.4 %multiply_reduce_fusion.3 = (f32[1024]{0:T(1024)S(1)}, f32[1024,1024]{0,1:T(8,128)S(1)}) fusion(bf16[1024,8192]{1,0:T(8,128)(2,1)} %get-tuple-element.371, s32[]{:T(128)S(6)} %select_n.19, f32[16,1024]{1,0:T(8,128)S(1)} %fusion.69, f32[1024,16]{0,1:T(8,128)S(1)} %get-tuple-element.373), kind=kOutput, calls=%fused_computation.1.clone.1 | convolution fusion | flops 205519872 | bytes 6426628 | tf_op jit(solution)/shard_map/while/body/eval_jaxpr/dot_general | solution.py:65
  273.1 2.6 fusion.70
  275.7 2.5 fusion.67
  279.9 5.4 %multiply_reduce_fusion.3 = (f32[1024]{0:T(1024)S(1)}, f32[1024,1024]{0,1:T(8,128)S(1)}) fusion(bf16[1024,8192]{1,0:T(8,128)(2,1)} %get-tuple-element.371, s32[]{:T(128)S(6)} %select_n.19, f32[16,1024]{1,0:T(8,128)S(1)} %fusion.69, f32[1024,16]{0,1:T(8,128)S(1)} %get-tuple-element.373), kind=kOutput, calls=%fused_computation.1.clone.1 | convolution fusion | flops 205519872 | bytes 6426628 | tf_op jit(solution)/shard_map/while/body/eval_jaxpr/dot_general | solution.py:65
  285.4 2.6 fusion.70
  288.0 2.5 fusion.67
  292.2 5.4 %multiply_reduce_fusion.3 = (f32[1024]{0:T(1024)S(1)}, f32[1024,1024]{0,1:T(8,128)S(1)}) fusion(bf16[1024,8192]{1,0:T(8,128)(2,1)} %get-tuple-element.371, s32[]{:T(128)S(6)} %select_n.19, f32[16,1024]{1,0:T(8,128)S(1)} %fusion.69, f32[1024,16]{0,1:T(8,128)S(1)} %get-tuple-element.373), kind=kOutput, calls=%fused_computation.1.clone.1 | convolution fusion | flops 205519872 | bytes 6426628 | tf_op jit(solution)/shard_map/while/body/eval_jaxpr/dot_general | solution.py:65
  297.6 2.6 fusion.70
  300.2 2.5 fusion.67
  304.5 5.4 %multiply_reduce_fusion.3 = (f32[1024]{0:T(1024)S(1)}, f32[1024,1024]{0,1:T(8,128)S(1)}) fusion(bf16[1024,8192]{1,0:T(8,128)(2,1)} %get-tuple-element.371, s32[]{:T(128)S(6)} %select_n.19, f32[16,1024]{1,0:T(8,128)S(1)} %fusion.69, f32[1024,16]{0,1:T(8,128)S(1)} %get-tuple-element.373), kind=kOutput, calls=%fused_computation.1.clone.1 | convolution fusion | flops 205519872 | bytes 6426628 | tf_op jit(solution)/shard_map/while/body/eval_jaxpr/dot_general | solution.py:65
  309.9 2.6 fusion.70
  (71 shorter events, 21.5 us)
Async XLA Ops:
  7.2 207.1 %all-gather.4.cloned.1.call-start = ((), (), s32[]{:S(2)}) async-start(), calls=%async_computation.1 | async-start | bytes 17039360 | tf_op jit(solution)/shard_map/all_gather | solution.py:41
  10.4 147.0 %all-to-all-start = ((f32[16,64,112]{2,0,1:T(8,128)}), f32[16,64,112]{2,0,1:T(8,128)S(1)}, u32[]{:S(2)}, u32[]{:S(2)}) async-start(f32[16,64,112]{2,0,1:T(8,128)} %copy.19), calls=%async_computation | async-start | bytes 1048576 | tf_op jit(solution)/shard_map/all_to_all | solution.py:42
Sparse Core Ops, SparseCore 0:
  9.9 204.3 all-gather.3
where the time goes:
time: 321 us; the launch traced here: 320 us
  blocking collectives  106 us (33%)
  matrix products  89.5 us (28%)
  waiting for transfers between devices  55.8 us (17%)
  starting transfers between devices  34.4 us (11%)
  other arithmetic  14.6 us (5%)
  between operations  14.1 us (4%)
  local copies, waits for them, and re-layouts  4.66 us (1%)
    all_gather x2, blocking collectives, gather_in_order(): parts = lax.all_gather(parts, axes[k])  106 us
    all_gather x1, waiting for transfers between devices, local(): dose_all = lax.all_gather(dosage, TILE, axis=0, tiled=True)  55.1 us
    dot_general x8, matrix products, one_block(): jnp.dot(covars_all, beta_dose, precision=highest, preferred_element_type=...  43.4 us
    all_to_all x1, starting transfers between devices, local(): lax.all_to_all(phenotypes, TILE, split_axis=1, concat_axis=0, tiled=True)  34.3 us
    dot_general x8, matrix products, one_block(): lax.dot_general(pheno_bf, dose_resid.astype(jnp.bfloat16), (((0,), (0,)),...  20.5 us
    dot_general x8, matrix products, one_block(): jnp.dot(covars_all.T, dose_block, precision=highest, preferred_element_ty...  20.1 us
    another operation x16, other arithmetic, one_block(): beta_dose = jax.scipy.linalg.cho_solve((factor, True), cov_dose)  9.88 us
  transfers between devices with their start and end apart: 2, of which 1 were waited for; matrix products, arithmetic and copies ran while one was open for 3% of the time, Pallas kernels for 0%

commit v1 on v0

v1 whole, which is shorter than its diff:
```python
import functools

import jax
import jax.numpy as jnp
from jax import lax
from jax.experimental import pallas as pl
from jax.experimental.pallas import tpu as pltpu
from jax.sharding import PartitionSpec as P

MESH = pl.DeviceIdType.MESH
LANES = 128
PIECES = 8
FIRST = 4
CW, CCW = 0, 1
F32, BF16 = jnp.float32, jnp.bfloat16


def split3(x):
    hi = x.astype(BF16)
    rest = x - hi.astype(F32)
    mid = rest.astype(BF16)
    lo = (rest - mid.astype(F32)).astype(BF16)
    return hi, mid, lo


def exact_dot(a, b):
    return jnp.dot(a, b, precision=lax.Precision.HIGHEST, preferred_element_type=F32)


def dot(a, b):
    return jnp.dot(a, b, preferred_element_type=F32)


def kernel(
    chips,
    genes,
    dose_ref,
    cov_ref,
    pheno_ref,
    chi_ref,
    hit_ref,
    dose_all,
    cov_all,
    pheno_all,
    stage,
    cw_box,
    ccw_box,
    cov_tile,
    cov_t,
    lhs,
    lhs_fix,
    small,
    gene_scale,
    chi_acc,
    hit_acc,
    mine,
    theirs,
    swap_send,
    swap_recv,
    own_sem,
    ring_send,
    ring_recv,
    ph_send,
    ph_recv,
    cv_send,
    cv_recv,
    pair_send,
    pair_recv,
):
    rows, variants = dose_ref.shape
    covs = cov_ref.shape[1]
    half = variants // 2
    width = half // PIECES
    pad = stage.shape[2]
    samples = rows * 2 * chips
    far = chips // 2
    near = chips - 1 - far

    me = lax.axis_index("tile")
    z, c = me // 2, lax.rem(me, 2)
    other = 1 - c
    partner = 2 * z + other
    right = 2 * lax.rem(z + 1, chips) + c
    left = 2 * lax.rem(z + chips - 1, chips) + c
    towards = (right, left)

    def source(direction, step):
        if direction == CW:
            return lax.rem(z + chips - step, chips)
        return lax.rem(z + step, chips)

    def hops(direction, piece):
        return far if (direction == CW) == (piece % 2 == 0) else near

    barrier = pltpu.get_barrier_semaphore()
    for peer in (partner, right, left):
        pl.semaphore_signal(barrier, inc=1, device_id={"tile": peer}, device_id_type=MESH)
    pl.semaphore_wait(barrier, 3)

    def swap(p):
        cols = pl.ds(pl.multiple_of(other * half + p * width, LANES), width)
        return pltpu.make_async_remote_copy(
            src_ref=dose_ref.at[:, cols],
            dst_ref=dose_all.at[p, z, c],
            send_sem=swap_send.at[p],
            recv_sem=swap_recv.at[p],
            device_id={"tile": partner},
            device_id_type=MESH,
        )

    def own(p):
        cols = pl.ds(pl.multiple_of(c * half + p * width, LANES), width)
        return pltpu.make_async_copy(dose_ref.at[:, cols], dose_all.at[p, z, c], own_sem.at[p])

    def ring(d, p, step, block):
        return pltpu.make_async_remote_copy(
            src_ref=dose_all.at[p, block],
            dst_ref=dose_all.at[p, block],
            send_sem=ring_send.at[d, p, step],
            recv_sem=ring_recv.at[d, p, step],
            device_id={"tile": towards[d]},
            device_id_type=MESH,
        )

    def ring_cov(d, step, block):
        return pltpu.make_async_remote_copy(
            src_ref=cov_all.at[block, c],
            dst_ref=cov_all.at[block, c],
            send_sem=cv_send.at[d, step],
            recv_sem=cv_recv.at[d, step],
            device_id={"tile": towards[d]},
            device_id_type=MESH,
        )

    reach = (far, near)
    boxes = (cw_box, ccw_box)

    def box_start(d, step):
        return sum(reach[d] - k for k in range(step))

    def ring_pheno(d, step):
        count = reach[d] - step
        if step == 0:
            src = stage.at[pl.ds(1, far)] if d == CW else stage.at[pl.ds(far + 1, near)]
        else:
            first = box_start(d, step - 1) + (1 if d == CW else 0)
            src = boxes[d].at[pl.ds(first, count)]
        return pltpu.make_async_remote_copy(
            src_ref=src,
            dst_ref=boxes[d].at[pl.ds(box_start(d, step), count)],
            send_sem=ph_send.at[d, step],
            recv_sem=ph_recv.at[d, step],
            device_id={"tile": towards[d]},
            device_id_type=MESH,
        )

    def keep_pheno(d, step):
        at = box_start(d, step) + (0 if d == CW else reach[d] - step - 1)
        pheno_all[source(d, step + 1), c] = boxes[d][at]

    for p in range(PIECES):
        swap(p).start()
        own(p).start()

    def launch(pieces):
        for p in pieces:
            own(p).wait()
            swap(p).wait_recv()
            for d in (CW, CCW):
                ring(d, p, 0, z).start()

    launch(range(FIRST))

    cov_tile[...] = jnp.zeros_like(cov_tile)
    cov_tile[:, 0:covs] = cov_ref[...]
    hi, mid, lo = split3(cov_tile[...])
    packed = (
        hi.astype(F32)
        + pltpu.roll(mid.astype(F32), covs, 1)
        + pltpu.roll(lo.astype(F32), 2 * covs, 1)
    )
    cov_all[z, c] = packed.astype(BF16)

    for j in range(chips):
        begin = genes * j
        base = begin // LANES * LANES
        wide = min(pad + LANES, pheno_ref.shape[1] - base)
        block = pheno_ref[:, base : base + wide]
        if begin > base:
            block = pltpu.roll(block, wide - (begin - base), 1)
        stage[lax.rem(j - z + chips, chips)] = block[:, :pad]

    for d in (CW, CCW):
        ring_cov(d, 0, z).start()
        ring_pheno(d, 0).start()
    pheno_all[z, c] = stage[0]
    chi_acc[...] = jnp.zeros_like(chi_acc)
    hit_acc[...] = jnp.zeros_like(hit_acc)

    def forward(p, step):
        for d in (CW, CCW):
            if step - 1 < hops(d, p):
                ring(d, p, step - 1, source(d, step)).wait_recv()
            if step < hops(d, p):
                ring(d, p, step, source(d, step)).start()

    for step in range(1, far + 1):
        if step == far:
            launch(range(FIRST, PIECES))
        for d in (CW, CCW):
            if step - 1 < reach[d]:
                ring_cov(d, step - 1, source(d, step)).wait_recv()
            if step < reach[d]:
                ring_cov(d, step, source(d, step)).start()
            if step - 1 < reach[d]:
                ring_pheno(d, step - 1).wait_recv()
            if step < reach[d]:
                ring_pheno(d, step).start()
            if step - 1 < reach[d]:
                keep_pheno(d, step - 1)
        for p in range(FIRST):
            forward(p, step)

    def pair_cov():
        return pltpu.make_async_remote_copy(
            src_ref=cov_all.at[:, c],
            dst_ref=cov_all.at[:, c],
            send_sem=pair_send.at[0],
            recv_sem=pair_recv.at[0],
            device_id={"tile": partner},
            device_id_type=MESH,
        )

    def pair_pheno():
        return pltpu.make_async_remote_copy(
            src_ref=pheno_all.at[:, c],
            dst_ref=pheno_all.at[:, c],
            send_sem=pair_send.at[1],
            recv_sem=pair_recv.at[1],
            device_id={"tile": partner},
            device_id_type=MESH,
        )

    pair_cov().start()
    pair_pheno().start()

    second = range(FIRST, PIECES)

    def forward_all(step):
        for p in second:
            forward(p, step)

    forward_all(1)
    pair_cov().wait_recv()
    cov2 = cov_all[...].reshape(samples, LANES)
    cov_t[...] = jnp.transpose(cov2.astype(F32)).astype(BF16)
    terms = 3 * covs
    lhs[genes : genes + terms] = cov_t[0:terms]
    pairs = dot(cov_t[...], cov2)
    pairs = pairs[0:covs] + pairs[covs : 2 * covs] + pairs[2 * covs : 3 * covs]
    pairs = pairs + pltpu.roll(pairs, LANES - covs, 1) + pltpu.roll(pairs, LANES - 2 * covs, 1)
    lane = lax.broadcasted_iota(jnp.int32, (covs, LANES), 1)
    row = lax.broadcasted_iota(jnp.int32, (covs, LANES), 0)
    gram_wide = jnp.where(lane < covs, pairs, 0.0)
    small[0] = gram_wide

    forward_all(2)

    def eliminate(k, a):
        column = jnp.sum(jnp.where(lane == k, a, 0.0), axis=1, keepdims=True)
        pivot_row = jnp.sum(jnp.where(row == k, a, 0.0), axis=0, keepdims=True)
        pivot = jnp.sum(jnp.where(lane[0:1] == k, pivot_row, 0.0), axis=1, keepdims=True)
        pivot_row = pivot_row / pivot
        return jnp.where(row == k, pivot_row, a - column * pivot_row)

    unit = jnp.where(lane == row + covs, 1.0, 0.0)
    solved = lax.fori_loop(0, covs, eliminate, gram_wide + unit)
    inverse = pltpu.roll(solved, LANES - covs, 1)[:, 0:covs]
    gram = gram_wide[:, 0:covs]
    eye = jnp.where(lane == row, 1.0, 0.0)[:, 0:covs]
    inverse = inverse + exact_dot(inverse, eye - exact_dot(gram, inverse))
    small[1, :, 0:covs] = inverse

    forward_all(3)
    pair_pheno().wait_recv()
    raw = pheno_all[...].reshape(samples, pad)
    cov_pheno = jnp.zeros((terms, pad), F32)
    for part in split3(raw):
        cov_pheno = cov_pheno + dot(cov_t[0:terms], part)
    cov_pheno = cov_pheno[0:covs] + cov_pheno[covs : 2 * covs] + cov_pheno[2 * covs : terms]
    beta = exact_dot(inverse, cov_pheno)
    blank = jnp.zeros((LANES - terms, pad), BF16)
    fit = jnp.zeros((samples, pad), F32)
    cov2 = cov_all[...].reshape(samples, LANES)
    for part in split3(beta):
        fit = fit + dot(cov2, jnp.concatenate([part, part, part, blank], axis=0))
    resid = jnp.transpose(pheno_all[...].reshape(samples, pad) - fit)[0:genes]
    forward_all(4)
    sumsq = jnp.sum(resid * resid, axis=1, keepdims=True)
    scale = 1.0 / (jnp.sqrt(F32(samples)) * jnp.sqrt(sumsq / samples + 0.1))
    gene_scale[...] = jnp.broadcast_to(scale, gene_scale.shape)
    lhs[0:genes] = resid.astype(BF16)
    fix = dot(lhs[0:genes], cov2)
    fix = fix + pltpu.roll(fix, LANES - covs, 1) + pltpu.roll(fix, LANES - 2 * covs, 1)
    fix_lane = lax.broadcasted_iota(jnp.int32, fix.shape, 1)
    lhs_fix[...] = jnp.where(fix_lane < covs, -fix, 0.0).astype(BF16)

    def scan(p):
        dose = dose_all[p].reshape(samples, width)
        both = dot(lhs[...], dose)
        cov_dose = (
            both[genes : genes + covs]
            + both[genes + covs : genes + 2 * covs]
            + both[genes + 2 * covs : genes + 3 * covs]
        )
        beta = exact_dot(small[1, :, 0:covs], cov_dose)
        back = exact_dot(small[0, :, 0:covs], beta)
        real = dose.astype(F32)
        dose_sumsq = jnp.sum(real * real, axis=0, keepdims=True) - jnp.sum(
            beta * (2.0 * cov_dose - back), axis=0, keepdims=True
        )
        dose_scale = 1.0 / jnp.sqrt(dose_sumsq / samples + 0.1)
        blank = jnp.zeros((LANES - covs, width), BF16)
        cross = both[0:genes] + dot(
            lhs_fix[...], jnp.concatenate([beta.astype(BF16), blank], axis=0)
        )
        scale = gene_scale[...]
        chi_sum, hit_sum = chi_acc[0:genes], hit_acc[0:genes]
        for n in range(width // LANES):
            cut = slice(n * LANES, (n + 1) * LANES)
            zscore = cross[:, cut] * dose_scale[:, cut] * scale
            chi = zscore * zscore
            chi_sum = chi_sum + chi
            hit_sum = hit_sum + 1.0 / (1.0 + jnp.exp(8.0 - 2.0 * chi))
        chi_acc[0:genes] = chi_sum
        hit_acc[0:genes] = hit_sum

    todo = list(range(FIRST))
    for step in range(5, far + 1):
        forward_all(step)
        if todo and step % 2 == 1:
            scan(todo.pop(0))
    lax.fori_loop(FIRST - len(todo), PIECES, lambda p, _: (scan(p), 0)[1], 0)

    mine[...] = jnp.zeros_like(mine)
    mine[0:1] = jnp.sum(jnp.transpose(chi_acc[...]), axis=0, keepdims=True)
    mine[1:2] = jnp.sum(jnp.transpose(hit_acc[...]), axis=0, keepdims=True)
    pair = pltpu.make_async_remote_copy(
        src_ref=mine,
        dst_ref=theirs,
        send_sem=pair_send.at[2],
        recv_sem=pair_recv.at[2],
        device_id={"tile": partner},
        device_id_type=MESH,
    )
    pair.start()
    for p in range(PIECES):
        swap(p).wait_send()
        for d in (CW, CCW):
            for step in range(hops(d, p)):
                ring(d, p, step, source(d, step)).wait_send()
    for d in (CW, CCW):
        for step in range(reach[d]):
            ring_cov(d, step, source(d, step)).wait_send()
            ring_pheno(d, step).wait_send()
    pair_cov().wait_send()
    pair_pheno().wait_send()
    pair.wait()
    total = mine[...] + theirs[...]
    own_genes = genes // 2
    total = jnp.where(c == 0, total, pltpu.roll(total, pad - own_genes, 1))
    chi_ref[...] = total[0:1, 0:own_genes] / variants
    hit_ref[...] = 20.0 / variants * total[1:2, 0:own_genes]


def local(dosage, covars, phenotypes):
    devices = lax.axis_size("tile")
    chips = devices // 2
    rows, variants = dosage.shape
    covs = covars.shape[1]
    genes = phenotypes.shape[1] // chips
    pad = -(-genes // LANES) * LANES
    samples = rows * devices
    width = variants // 2 // PIECES
    far = chips // 2
    near = chips - 1 - far
    dma = pltpu.SemaphoreType.DMA
    vmem = pltpu.VMEM
    scratch = [
        vmem((PIECES, chips, 2, rows, width), BF16),
        vmem((chips, 2, rows, LANES), BF16),
        vmem((chips, 2, rows, pad), F32),
        vmem((chips, rows, pad), F32),
        vmem((far * (far + 1) // 2, rows, pad), F32),
        vmem((near * (near + 1) // 2, rows, pad), F32),
        vmem((rows, LANES), F32),
        vmem((LANES, samples), BF16),
        vmem((genes + 3 * covs, samples), BF16),
        vmem((genes, LANES), BF16),
        vmem((2, covs, LANES), F32),
        vmem((genes, LANES), F32),
        vmem((pad, LANES), F32),
        vmem((pad, LANES), F32),
        vmem((8, pad), F32),
        vmem((8, pad), F32),
        dma((PIECES,)),
        dma((PIECES,)),
        dma((PIECES,)),
        dma((2, PIECES, far)),
        dma((2, PIECES, far)),
        dma((2, far)),
        dma((2, far)),
        dma((2, far)),
        dma((2, far)),
        dma((3,)),
        dma((3,)),
    ]
    whole = pl.BlockSpec(memory_space=pltpu.VMEM)
    own_genes = genes // 2
    chi, hit = pl.pallas_call(
        functools.partial(kernel, chips, genes),
        out_shape=[jax.ShapeDtypeStruct((1, own_genes), F32)] * 2,
        in_specs=[whole] * 3,
        out_specs=[whole] * 2,
        scratch_shapes=scratch,
        compiler_params=pltpu.CompilerParams(
            collective_id=0, has_side_effects=True, vmem_limit_bytes=48 * 2**20
        ),
    )(dosage, covars, phenotypes)
    return chi.reshape(own_genes), hit.reshape(own_genes)


def solution(mesh):
    rows = P(("cohort", "tile"), None)
    return jax.shard_map(
        local,
        mesh=mesh,
        in_specs=(rows, rows, rows),
        out_specs=(P(("cohort", "tile")), P(("cohort", "tile"))),
        check_vma=False,
    )
```

time: 321 us -> 193 us (0.60)
  Pallas kernels: 0 us -> 188 us
  blocking collectives: 106 us -> 0 us
  matrix products: 89.5 us -> 0 us
  waiting for transfers between devices: 55.8 us -> 0 us
  starting transfers between devices: 34.4 us -> 0 us
  other arithmetic: 14.6 us -> 0 us
  between operations: 14.1 us -> 0.65 us
    pallas_call x0 -> x1, Pallas kernels: none -> 188 us  [local(): pl.pallas_call(functools.partial(kernel, chips, genes), out_shape=[jax.Sh...]
    all_gather x2 -> x0, blocking collectives: 106 us -> none  [gather_in_order(): parts = lax.all_gather(parts, axes[k])]
    dot_general x27 -> x0, matrix products: 85.5 us -> none  [the longest x8 43.4 us: one_block(): jnp.dot(covars_all, beta_dose, precision=highest, preferred_element_type=...]
    all_gather x1 -> x0, waiting for transfers between devices: 55.1 us -> none  [local(): dose_all = lax.all_gather(dosage, TILE, axis=0, tiled=True)]
    all_to_all x1 -> x0, starting transfers between devices: 34.3 us -> none  [local(): lax.all_to_all(phenotypes, TILE, split_axis=1, concat_axis=0, tiled=True)]
    another operation x21 -> x0, other arithmetic: 13.9 us -> none  [the longest x16 9.88 us: one_block(): beta_dose = jax.scipy.linalg.cho_solve((factor, True), cov_dose)]
    another operation x18 -> x0, matrix products: 4.03 us -> none  [the longest x16 3.69 us: one_block(): beta_dose = jax.scipy.linalg.cho_solve((factor, True), cov_dose)]
    unnamed x1 -> x8, local copies, waits for them, and re-layouts: 0.18 us -> 3.68 us
  transfers between devices with their start and end apart: 2 -> 0, of which waited for: 1 -> 0; matrix products, arithmetic and copies ran while one was open for 3% -> 0% of each run, Pallas kernels for 0% -> 0%
where the time goes in v1:
time: 193 us
  Pallas kernels  188 us (97%)
  local copies, waits for them, and re-layouts  3.68 us (2%)
    pallas_call x1, Pallas kernels, local(): pl.pallas_call(functools.partial(kernel, chips, genes), out_shape=[jax.Sh...  188 us

profile of v1, /device:TPU:37, one launch (start us, length us, event | category | flops | bytes accessed | tf_op | source)
XLA Modules:
  0.0 192.8 jit_solution(14455789478882758881)
XLA Ops:
  0.6 0.0 copy-start
  0.6 1.0 copy-done
  1.6 0.0 copy-start.1
  1.7 0.9 copy-done.1
  2.6 0.0 copy-start.2
  2.6 0.7 copy-done.2
  3.3 188.5 %shard_map.50 = (f32[1,112]{1,0:T(1,128)S(1)}, f32[1,112]{1,0:T(1,128)S(1)}) custom-call(bf16[16,8192]{1,0:T(8,128)(2,1)S(1)} %copy-done.1, f32[16,16]{1,0:T(8,128)S(1)} %copy-done.2, f32[16,7168]{1,0:T(8,128)S(1)} %copy-done), custom_call_target="tpu_custom_call" | custom-call | tf_op jit(solution)/shard_map/pallas_call | solution.py:420
  191.8 0.5 copy.7
  192.3 0.5 copy.8
Async XLA Ops:
  0.6 1.0 copy-start
  1.6 0.9 copy-start.1
  2.6 0.7 copy-start.2

commit v2 on v1

v2 whole, which is shorter than its diff:
```python
import functools

import jax
import jax.numpy as jnp
from jax import lax
from jax.experimental import pallas as pl
from jax.experimental.pallas import tpu as pltpu
from jax.sharding import PartitionSpec as P

MESH = pl.DeviceIdType.MESH
LANES = 128
PIECES = 8
START = (0, 0, 0, 8, 8, 8, 8, 8)
PHENO_TICK = 2
CW, CCW = 0, 1
F32, BF16 = jnp.float32, jnp.bfloat16


def split3(x):
    hi = x.astype(BF16)
    rest = x - hi.astype(F32)
    mid = rest.astype(BF16)
    lo = (rest - mid.astype(F32)).astype(BF16)
    return hi, mid, lo


def exact_dot(a, b):
    return jnp.dot(a, b, precision=lax.Precision.HIGHEST, preferred_element_type=F32)


def dot(a, b):
    return jnp.dot(a, b, preferred_element_type=F32)


def kernel(
    chips,
    genes,
    dose_hbm,
    cov_hbm,
    pheno_hbm,
    chi_ref,
    hit_ref,
    dose_ref,
    cov_ref,
    pheno_ref,
    dose_all,
    cov_all,
    pheno_all,
    stage,
    chip_raw,
    out_box,
    cw_box,
    ccw_box,
    kept,
    cov_tile,
    chip_tile,
    cov_t,
    lhs,
    lhs_fix,
    small,
    gene_scale,
    chi_acc,
    hit_acc,
    mine,
    theirs,
    load_sem,
    swap_send,
    swap_recv,
    own_sem,
    raw_sem,
    ring_send,
    ring_recv,
    ph_send,
    ph_recv,
    cv_send,
    cv_recv,
    pair_send,
    pair_recv,
):
    rows, variants = dose_ref.shape
    covs = cov_ref.shape[1]
    half = variants // 2
    width = half // PIECES
    own_genes = genes // 2
    pad = kept.shape[2]
    samples = rows * 2 * chips
    far = chips // 2
    near = chips - 1 - far

    me = lax.axis_index("tile")
    z, c = me // 2, lax.rem(me, 2)
    other = 1 - c
    partner = 2 * z + other
    right = 2 * lax.rem(z + 1, chips) + c
    left = 2 * lax.rem(z + chips - 1, chips) + c
    towards = (right, left)

    def source(direction, step):
        if direction == CW:
            return lax.rem(z + chips - step, chips)
        return lax.rem(z + step, chips)

    def hops(direction, piece):
        return far if (direction == CW) == (piece == 0) else near

    loads = [
        pltpu.make_async_copy(src, dst, load_sem.at[k])
        for k, (src, dst) in enumerate(
            ((dose_hbm, dose_ref), (cov_hbm, cov_ref), (pheno_hbm, pheno_ref))
        )
    ]
    for copy in loads:
        copy.start()
    barrier = pltpu.get_barrier_semaphore()
    for peer in (partner, right, left):
        pl.semaphore_signal(barrier, inc=1, device_id={"tile": peer}, device_id_type=MESH)
    pl.semaphore_wait(barrier, 3)
    for copy in loads:
        copy.wait()

    def swap(p):
        cols = pl.ds(pl.multiple_of(other * half + p * width, LANES), width)
        return pltpu.make_async_remote_copy(
            src_ref=dose_ref.at[:, cols],
            dst_ref=dose_all.at[p, z, c],
            send_sem=swap_send.at[p],
            recv_sem=swap_recv.at[p],
            device_id={"tile": partner},
            device_id_type=MESH,
        )

    def own(p):
        cols = pl.ds(pl.multiple_of(c * half + p * width, LANES), width)
        return pltpu.make_async_copy(dose_ref.at[:, cols], dose_all.at[p, z, c], own_sem.at[p])

    def ring(d, p, step, block):
        return pltpu.make_async_remote_copy(
            src_ref=dose_all.at[p, block],
            dst_ref=dose_all.at[p, block],
            send_sem=ring_send.at[d, p, step],
            recv_sem=ring_recv.at[d, p, step],
            device_id={"tile": towards[d]},
            device_id_type=MESH,
        )

    def ring_cov(d, step, block):
        return pltpu.make_async_remote_copy(
            src_ref=cov_all.at[block, c],
            dst_ref=cov_all.at[block, c],
            send_sem=cv_send.at[d, step],
            recv_sem=cv_recv.at[d, step],
            device_id={"tile": towards[d]},
            device_id_type=MESH,
        )

    reach = (far, near)
    boxes = (cw_box, ccw_box)

    def box_start(d, step):
        return sum(reach[d] - k for k in range(step))

    def ring_pheno(d, step):
        count = reach[d] - step
        if step == 0:
            src = out_box.at[pl.ds(1, far)] if d == CW else out_box.at[pl.ds(far + 1, near)]
        else:
            first = box_start(d, step - 1) + (1 if d == CW else 0)
            src = boxes[d].at[pl.ds(first, count)]
        return pltpu.make_async_remote_copy(
            src_ref=src,
            dst_ref=boxes[d].at[pl.ds(box_start(d, step), count)],
            send_sem=ph_send.at[d, step],
            recv_sem=ph_recv.at[d, step],
            device_id={"tile": towards[d]},
            device_id_type=MESH,
        )

    def keep_pheno(d, step):
        at = box_start(d, step) + (0 if d == CW else reach[d] - step - 1)
        kept[source(d, step + 1)] = boxes[d][at]

    for p in range(PIECES):
        swap(p).start()
        own(p).start()

    def launch(pieces):
        for p in pieces:
            own(p).wait()
            swap(p).wait_recv()
            for d in (CW, CCW):
                ring(d, p, 0, z).start()

    def tick_of(p):
        return START[p] * far // 16

    launch([p for p in range(PIECES) if tick_of(p) == 0])

    cov_tile[...] = jnp.zeros_like(cov_tile)
    cov_tile[:, 0:covs] = cov_ref[...]
    hi, mid, lo = split3(cov_tile[...])
    packed = (
        hi.astype(F32)
        + pltpu.roll(mid.astype(F32), covs, 1)
        + pltpu.roll(lo.astype(F32), 2 * covs, 1)
    )
    cov_all[z, c] = packed.astype(BF16)
    chip_tile[c] = packed.astype(BF16)

    for j in range(chips):
        place = pl.ds(pl.multiple_of(lax.rem(j - z + chips, chips) * pad, LANES), pad)
        for h in range(2):
            begin = genes * j + own_genes * h
            base = begin // LANES * LANES
            wide = min(pad + LANES, pheno_ref.shape[1] - base)
            block = pheno_ref[:, base : base + wide]
            if begin > base:
                block = pltpu.roll(block, wide - (begin - base), 1)
            stage[h, :, place] = block[:, :pad]

    def pair(slot, src, dst):
        return pltpu.make_async_remote_copy(
            src_ref=src,
            dst_ref=dst,
            send_sem=pair_send.at[slot],
            recv_sem=pair_recv.at[slot],
            device_id={"tile": partner},
            device_id_type=MESH,
        )

    pair_tile = pair(0, chip_tile.at[c], chip_tile.at[c])
    pair_raw = pair(1, stage.at[other], chip_raw.at[c])
    own_raw = pltpu.make_async_copy(stage.at[c], chip_raw.at[c], raw_sem)
    pair_tile.start()
    pair_raw.start()
    own_raw.start()
    for d in (CW, CCW):
        ring_cov(d, 0, z).start()
    chi_acc[...] = jnp.zeros_like(chi_acc)
    hit_acc[...] = jnp.zeros_like(hit_acc)

    lane = lax.broadcasted_iota(jnp.int32, (covs, LANES), 1)
    row = lax.broadcasted_iota(jnp.int32, (covs, LANES), 0)
    terms = 3 * covs

    def three_rows(x):
        return x[0:covs] + x[covs : 2 * covs] + x[2 * covs : terms]

    def three_lanes(x):
        return x + pltpu.roll(x, LANES - covs, 1) + pltpu.roll(x, LANES - 2 * covs, 1)

    def gram_of(x, x_t):
        return jnp.where(lane < covs, three_lanes(three_rows(dot(x_t, x))), 0.0)

    def eliminate(k, a):
        column = jnp.sum(jnp.where(lane == k, a, 0.0), axis=1, keepdims=True)
        pivot_row = jnp.sum(jnp.where(row == k, a, 0.0), axis=0, keepdims=True)
        pivot = jnp.sum(jnp.where(lane[0:1] == k, pivot_row, 0.0), axis=1, keepdims=True)
        pivot_row = pivot_row / pivot
        return jnp.where(row == k, pivot_row, a - column * pivot_row)

    def invert(wide_gram):
        unit = jnp.where(lane == row + covs, 1.0, 0.0)
        solved = lax.fori_loop(0, covs, eliminate, wide_gram + unit)
        return pltpu.roll(solved, LANES - covs, 1)[:, 0:covs]

    def thrice(x):
        blank = jnp.zeros((LANES - terms, x.shape[1]), BF16)
        return jnp.concatenate([x, x, x, blank], axis=0)

    def prepare_pheno():
        pair_tile.wait_recv()
        chip_cov = chip_tile[...].reshape(2 * rows, LANES)
        chip_cov_t = jnp.transpose(chip_cov.astype(F32))
        chip_gram = gram_of(chip_cov, chip_cov_t.astype(BF16))
        ridge = jnp.where(lane == row, chip_gram * 1e-4 + 1e-6, 0.0)
        solve = exact_dot(invert(chip_gram + ridge), three_rows(chip_cov_t))
        solve_hi = solve.astype(BF16)
        solve_lo = (solve - solve_hi.astype(F32)).astype(BF16)
        solver = jnp.concatenate([solve_hi, solve_lo], axis=0)
        own_raw.wait()
        pair_raw.wait_recv()
        group = 8 * pad

        def fit_group(g, carry):
            place = pl.ds(pl.multiple_of(g * group, LANES), group)
            raw = chip_raw[:, :, place].reshape(2 * rows, group)
            both = dot(solver, raw.astype(BF16))
            beta = (both[0:covs] + both[covs : 2 * covs]).astype(BF16)
            left_over = (raw - dot(chip_cov, thrice(beta))).astype(BF16)
            for k in range(8):
                cut = slice(k * pad, (k + 1) * pad)
                out_box[g * 8 + k, 0 : 2 * rows] = left_over[:, cut]
                out_box[g * 8 + k, 2 * rows : 2 * rows + covs] = beta[:, cut]
            return carry

        lax.fori_loop(0, chips // 8, fit_group, 0)

    def launch_pheno():
        for d in (CW, CCW):
            ring_pheno(d, 0).start()
        kept[z] = out_box[0]

    def forward(p, step):
        for d in (CW, CCW):
            if 0 <= step - 1 < hops(d, p):
                ring(d, p, step - 1, source(d, step)).wait_recv()
            if 0 < step < hops(d, p):
                ring(d, p, step, source(d, step)).start()

    sent_at = max(1, PHENO_TICK * far // 16)

    def tick(t):
        launch([p for p in range(PIECES) if t > 0 and tick_of(p) == t])
        for d in (CW, CCW):
            if 0 < t <= reach[d]:
                ring_cov(d, t - 1, source(d, t)).wait_recv()
            if 0 < t < reach[d]:
                ring_cov(d, t, source(d, t)).start()
        step = t - sent_at
        for d in (CW, CCW):
            if 0 < step <= reach[d]:
                ring_pheno(d, step - 1).wait_recv()
            if 0 < step < reach[d]:
                ring_pheno(d, step).start()
            if 0 < step <= reach[d]:
                keep_pheno(d, step - 1)
        for p in sorted(range(PIECES), key=tick_of):
            if 0 < t - tick_of(p) <= far:
                forward(p, t - tick_of(p))

    last = max([tick_of(p) for p in range(PIECES)] + [sent_at + 1]) + far
    pending = list(range(1, last + 1))

    def next_tick():
        if pending:
            tick(pending.pop(0))

    for _ in range(sent_at):
        next_tick()
    prepare_pheno()
    launch_pheno()
    for _ in range(far):
        next_tick()

    pair_cov = pair(2, cov_all.at[:, c], cov_all.at[:, c])
    pair_cov.start()

    next_tick()
    pair_cov.wait_recv()
    cov2 = cov_all[...].reshape(samples, LANES)
    cov_t[...] = jnp.transpose(cov2.astype(F32)).astype(BF16)
    lhs[genes : genes + terms] = cov_t[0:terms]
    gram_wide = gram_of(cov2, cov_t[...])
    small[0] = gram_wide
    inverse = invert(gram_wide)
    eye = jnp.where(lane == row, 1.0, 0.0)[:, 0:covs]
    inverse = inverse + exact_dot(inverse, eye - exact_dot(gram_wide[:, 0:covs], inverse))
    small[1, :, 0:covs] = inverse
    next_tick()

    for k in range(chips):
        block = kept[k]
        fitted = dot(cov_all[k].reshape(2 * rows, LANES), thrice(block[2 * rows :]))
        pheno_all[pl.ds(k * 2 * rows, 2 * rows)] = block[0 : 2 * rows].astype(F32) + fitted
    next_tick()
    cov_pheno = jnp.zeros((terms, pad), F32)
    for part in split3(pheno_all[...]):
        cov_pheno = cov_pheno + dot(cov_t[0:terms], part)
    beta = exact_dot(inverse, three_rows(cov_pheno))
    fit = jnp.zeros((samples, pad), F32)
    cov2 = cov_all[...].reshape(samples, LANES)
    for part in split3(beta):
        fit = fit + dot(cov2, thrice(part))
    resid = jnp.transpose(pheno_all[...] - fit)[0:own_genes]
    sumsq = jnp.sum(resid * resid, axis=1, keepdims=True)
    scale = 1.0 / (jnp.sqrt(F32(samples)) * jnp.sqrt(sumsq / samples + 0.1))
    resid_bf = resid.astype(BF16)
    fix = three_lanes(dot(resid_bf, cov2))
    fix_lane = lax.broadcasted_iota(jnp.int32, fix.shape, 1)
    mine_rows = pl.ds(pl.multiple_of(c * own_genes, 16), own_genes)
    lhs[mine_rows] = resid_bf
    lhs_fix[mine_rows] = jnp.where(fix_lane < covs, -fix, 0.0).astype(BF16)
    gene_scale[mine_rows] = jnp.broadcast_to(scale, (own_genes, LANES))
    next_tick()
    pair_rows = [
        pair(3 + k, ref.at[mine_rows], ref.at[mine_rows])
        for k, ref in enumerate((lhs, lhs_fix, gene_scale))
    ]
    for copy in pair_rows:
        copy.start()
    next_tick()
    for copy in pair_rows:
        copy.wait_recv()

    def scan(p):
        dose = dose_all[p].reshape(samples, width)
        both = dot(lhs[...], dose)
        cov_dose = (
            both[genes : genes + covs]
            + both[genes + covs : genes + 2 * covs]
            + both[genes + 2 * covs : genes + 3 * covs]
        )
        beta = exact_dot(small[1, :, 0:covs], cov_dose)
        back = exact_dot(small[0, :, 0:covs], beta)
        real = dose.astype(F32)
        dose_sumsq = jnp.sum(real * real, axis=0, keepdims=True) - jnp.sum(
            beta * (2.0 * cov_dose - back), axis=0, keepdims=True
        )
        dose_scale = 1.0 / jnp.sqrt(dose_sumsq / samples + 0.1)
        blank = jnp.zeros((LANES - covs, width), BF16)
        cross = both[0:genes] + dot(
            lhs_fix[...], jnp.concatenate([beta.astype(BF16), blank], axis=0)
        )
        scale = gene_scale[...]
        chi_sum, hit_sum = chi_acc[0:genes], hit_acc[0:genes]
        for n in range(width // LANES):
            cut = slice(n * LANES, (n + 1) * LANES)
            zscore = cross[:, cut] * dose_scale[:, cut] * scale
            chi = zscore * zscore
            chi_sum = chi_sum + chi
            hit_sum = hit_sum + 1.0 / (1.0 + jnp.exp(8.0 - 2.0 * chi))
        chi_acc[0:genes] = chi_sum
        hit_acc[0:genes] = hit_sum

    done = 0
    while pending:
        now = pending[0]
        next_tick()
        if done < PIECES and tick_of(done) + far < now:
            scan(done)
            done += 1
    lax.fori_loop(done, PIECES, lambda p, _: (scan(p), 0)[1], 0)

    mine[...] = jnp.zeros_like(mine)
    mine[0:1] = jnp.sum(jnp.transpose(chi_acc[...]), axis=0, keepdims=True)
    mine[1:2] = jnp.sum(jnp.transpose(hit_acc[...]), axis=0, keepdims=True)
    pair_sums = pair(6, mine, theirs)
    pair_sums.start()
    for p in range(PIECES):
        swap(p).wait_send()
        for d in (CW, CCW):
            for step in range(hops(d, p)):
                ring(d, p, step, source(d, step)).wait_send()
    for d in (CW, CCW):
        for step in range(reach[d]):
            ring_cov(d, step, source(d, step)).wait_send()
            ring_pheno(d, step).wait_send()
    for copy in (pair_tile, pair_raw, pair_cov, *pair_rows):
        copy.wait_send()
    pair_sums.wait()
    total = mine[...] + theirs[...]
    total = jnp.where(c == 0, total, pltpu.roll(total, total.shape[1] - own_genes, 1))
    chi_ref[...] = total[0:1, 0:own_genes] / variants
    hit_ref[...] = 20.0 / variants * total[1:2, 0:own_genes]


def local(dosage, covars, phenotypes):
    devices = lax.axis_size("tile")
    chips = devices // 2
    rows, variants = dosage.shape
    covs = covars.shape[1]
    genes = phenotypes.shape[1] // chips
    own_genes = genes // 2
    pad = -(-own_genes // LANES) * LANES
    wide = -(-genes // LANES) * LANES
    sent = 2 * rows + covs
    samples = rows * devices
    width = variants // 2 // PIECES
    far = chips // 2
    near = chips - 1 - far
    dma = pltpu.SemaphoreType.DMA
    vmem = pltpu.VMEM
    scratch = [
        vmem(dosage.shape, BF16),
        vmem(covars.shape, F32),
        vmem(phenotypes.shape, F32),
        vmem((PIECES, chips, 2, rows, width), BF16),
        vmem((chips, 2, rows, LANES), BF16),
        vmem((samples, pad), F32),
        vmem((2, rows, chips * pad), F32),
        vmem((2, rows, chips * pad), F32),
        vmem((chips, sent, pad), BF16),
        vmem((far * (far + 1) // 2, sent, pad), BF16),
        vmem((near * (near + 1) // 2, sent, pad), BF16),
        vmem((chips, sent, pad), BF16),
        vmem((rows, LANES), F32),
        vmem((2, rows, LANES), BF16),
        vmem((LANES, samples), BF16),
        vmem((genes + 3 * covs, samples), BF16),
        vmem((genes, LANES), BF16),
        vmem((2, covs, LANES), F32),
        vmem((genes, LANES), F32),
        vmem((wide, LANES), F32),
        vmem((wide, LANES), F32),
        vmem((8, wide), F32),
        vmem((8, wide), F32),
        dma((3,)),
        dma((PIECES,)),
        dma((PIECES,)),
        dma((PIECES,)),
        dma(()),
        dma((2, PIECES, far)),
        dma((2, PIECES, far)),
        dma((2, far)),
        dma((2, far)),
        dma((2, far)),
        dma((2, far)),
        dma((7,)),
        dma((7,)),
    ]
    whole = pl.BlockSpec(memory_space=pltpu.VMEM)
    chi, hit = pl.pallas_call(
        functools.partial(kernel, chips, genes),
        out_shape=[jax.ShapeDtypeStruct((1, own_genes), F32)] * 2,
        in_specs=[pl.BlockSpec(memory_space=pltpu.HBM)] * 3,
        out_specs=[whole] * 2,
        scratch_shapes=scratch,
        compiler_params=pltpu.CompilerParams(
            collective_id=0, has_side_effects=True, vmem_limit_bytes=48 * 2**20
        ),
    )(dosage, covars, phenotypes)
    return chi.reshape(own_genes), hit.reshape(own_genes)


def solution(mesh):
    rows = P(("cohort", "tile"), None)
    return jax.shard_map(
        local,
        mesh=mesh,
        in_specs=(rows, rows, rows),
        out_specs=(P(("cohort", "tile")), P(("cohort", "tile"))),
        check_vma=False,
    )
```

time: 193 us -> 182 us (0.943)
  Pallas kernels: 188 us -> 178 us
    pallas_call x1, Pallas kernels: 188 us -> 178 us  [local(): pl.pallas_call(functools.partial(kernel, chips, genes), out_shape=[jax.Sh...]
where the time goes in v2:
time: 182 us
  Pallas kernels  178 us (98%)
  local copies, waits for them, and re-layouts  3.68 us (2%)
    pallas_call x1, Pallas kernels, local(): pl.pallas_call(functools.partial(kernel, chips, genes), out_shape=[jax.Sh...  178 us
    unnamed x8, local copies, waits for them, and re-layouts  3.68 us

profile of v2, /device:TPU:37, one launch (start us, length us, event | category | flops | bytes accessed | tf_op | source)
XLA Modules:
  0.0 182.0 jit_solution(9580849985636814366)
XLA Ops:
  0.6 0.0 copy-start
  0.6 1.0 copy-done
  1.6 0.0 copy-start.1
  1.7 0.9 copy-done.1
  2.6 0.0 copy-start.2
  2.6 0.7 copy-done.2
  3.3 177.7 %shard_map.50 = (f32[1,112]{1,0:T(1,128)S(1)}, f32[1,112]{1,0:T(1,128)S(1)}) custom-call(bf16[16,8192]{1,0:T(8,128)(2,1)S(1)} %copy-done.1, f32[16,16]{1,0:T(8,128)S(1)} %copy-done.2, f32[16,7168]{1,0:T(8,128)S(1)} %copy-done), custom_call_target="tpu_custom_call" | custom-call | tf_op jit(solution)/shard_map/pallas_call | solution.py:512
  181.0 0.5 copy.7
  181.5 0.5 copy.8
Async XLA Ops:
  0.6 1.0 copy-start
  1.6 0.9 copy-start.1
  2.6 0.7 copy-start.2

commit v3 on v2

--- a/solution.py
+++ b/solution.py
@@ -10,8 +10,8 @@
 MESH = pl.DeviceIdType.MESH
 LANES = 128
 PIECES = 8
-START = (0, 0, 0, 8, 8, 8, 8, 8)
-PHENO_TICK = 2
+START = (0, 0, 0, 9, 9, 9, 9, 9)
+PHENO_TICK = 1
 CW, CCW = 0, 1
 F32, BF16 = jnp.float32, jnp.bfloat16
 
@@ -59,6 +59,8 @@
     lhs_fix,
     small,
     gene_scale,
+    partial,
+    partial_sq,
     chi_acc,
     hit_acc,
     mine,
@@ -95,10 +97,8 @@
     left = 2 * lax.rem(z + chips - 1, chips) + c
     towards = (right, left)
 
-    def source(direction, step):
-        if direction == CW:
-            return lax.rem(z + chips - step, chips)
-        return lax.rem(z + step, chips)
+    def slot(direction, step):
+        return (chips - step) % chips if direction == CW else step
 
     def hops(direction, piece):
         return far if (direction == CW) == (piece == 0) else near
@@ -122,7 +122,7 @@
         cols = pl.ds(pl.multiple_of(other * half + p * width, LANES), width)
         return pltpu.make_async_remote_copy(
             src_ref=dose_ref.at[:, cols],
-            dst_ref=dose_all.at[p, z, c],
+            dst_ref=dose_all.at[p, 0, c],
             send_sem=swap_send.at[p],
             recv_sem=swap_recv.at[p],
             device_id={"tile": partner},
@@ -131,22 +131,22 @@
 
     def own(p):
         cols = pl.ds(pl.multiple_of(c * half + p * width, LANES), width)
-        return pltpu.make_async_copy(dose_ref.at[:, cols], dose_all.at[p, z, c], own_sem.at[p])
-
-    def ring(d, p, step, block):
+        return pltpu.make_async_copy(dose_ref.at[:, cols], dose_all.at[p, 0, c], own_sem.at[p])
+
+    def ring(d, p, step):
         return pltpu.make_async_remote_copy(
-            src_ref=dose_all.at[p, block],
-            dst_ref=dose_all.at[p, block],
+            src_ref=dose_all.at[p, slot(d, step)],
+            dst_ref=dose_all.at[p, slot(d, step + 1)],
             send_sem=ring_send.at[d, p, step],
             recv_sem=ring_recv.at[d, p, step],
             device_id={"tile": towards[d]},
             device_id_type=MESH,
         )
 
-    def ring_cov(d, step, block):
+    def ring_cov(d, step):
         return pltpu.make_async_remote_copy(
-            src_ref=cov_all.at[block, c],
-            dst_ref=cov_all.at[block, c],
+            src_ref=cov_all.at[slot(d, step), c],
+            dst_ref=cov_all.at[slot(d, step + 1), c],
             send_sem=cv_send.at[d, step],
             recv_sem=cv_recv.at[d, step],
             device_id={"tile": towards[d]},
@@ -177,7 +177,7 @@
 
     def keep_pheno(d, step):
         at = box_start(d, step) + (0 if d == CW else reach[d] - step - 1)
-        kept[source(d, step + 1)] = boxes[d][at]
+        kept[slot(d, step + 1)] = boxes[d][at]
 
     for p in range(PIECES):
         swap(p).start()
@@ -188,7 +188,7 @@
             own(p).wait()
             swap(p).wait_recv()
             for d in (CW, CCW):
-                ring(d, p, 0, z).start()
+                ring(d, p, 0).start()
 
     def tick_of(p):
         return START[p] * far // 16
@@ -203,7 +203,7 @@
         + pltpu.roll(mid.astype(F32), covs, 1)
         + pltpu.roll(lo.astype(F32), 2 * covs, 1)
     )
-    cov_all[z, c] = packed.astype(BF16)
+    cov_all[0, c] = packed.astype(BF16)
     chip_tile[c] = packed.astype(BF16)
 
     for j in range(chips):
@@ -234,7 +234,7 @@
     pair_raw.start()
     own_raw.start()
     for d in (CW, CCW):
-        ring_cov(d, 0, z).start()
+        ring_cov(d, 0).start()
     chi_acc[...] = jnp.zeros_like(chi_acc)
     hit_acc[...] = jnp.zeros_like(hit_acc)
 
@@ -277,6 +277,7 @@
         solve_hi = solve.astype(BF16)
         solve_lo = (solve - solve_hi.astype(F32)).astype(BF16)
         solver = jnp.concatenate([solve_hi, solve_lo], axis=0)
+        next_tick()
         own_raw.wait()
         pair_raw.wait_recv()
         group = 8 * pad
@@ -293,29 +294,32 @@
                 out_box[g * 8 + k, 2 * rows : 2 * rows + covs] = beta[:, cut]
             return carry
 
-        lax.fori_loop(0, chips // 8, fit_group, 0)
+        half_groups = chips // 16
+        lax.fori_loop(0, half_groups, fit_group, 0)
+        next_tick()
+        lax.fori_loop(half_groups, chips // 8, fit_group, 0)
 
     def launch_pheno():
         for d in (CW, CCW):
             ring_pheno(d, 0).start()
-        kept[z] = out_box[0]
+        kept[0] = out_box[0]
 
     def forward(p, step):
         for d in (CW, CCW):
             if 0 <= step - 1 < hops(d, p):
-                ring(d, p, step - 1, source(d, step)).wait_recv()
+                ring(d, p, step - 1).wait_recv()
             if 0 < step < hops(d, p):
-                ring(d, p, step, source(d, step)).start()
-
-    sent_at = max(1, PHENO_TICK * far // 16)
+                ring(d, p, step).start()
+
+    sent_at = 2 + PHENO_TICK
 
     def tick(t):
         launch([p for p in range(PIECES) if t > 0 and tick_of(p) == t])
         for d in (CW, CCW):
             if 0 < t <= reach[d]:
-                ring_cov(d, t - 1, source(d, t)).wait_recv()
+                ring_cov(d, t - 1).wait_recv()
             if 0 < t < reach[d]:
-                ring_cov(d, t, source(d, t)).start()
+                ring_cov(d, t).start()
         step = t - sent_at
         for d in (CW, CCW):
             if 0 < step <= reach[d]:
@@ -331,15 +335,18 @@
     last = max([tick_of(p) for p in range(PIECES)] + [sent_at + 1]) + far
     pending = list(range(1, last + 1))
 
+    def now():
+        return pending[0] if pending else last + 1
+
     def next_tick():
         if pending:
             tick(pending.pop(0))
 
-    for _ in range(sent_at):
+    for _ in range(sent_at - 2):
         next_tick()
     prepare_pheno()
     launch_pheno()
-    for _ in range(far):
+    while now() <= far:
         next_tick()
 
     pair_cov = pair(2, cov_all.at[:, c], cov_all.at[:, c])
@@ -356,13 +363,13 @@
     eye = jnp.where(lane == row, 1.0, 0.0)[:, 0:covs]
     inverse = inverse + exact_dot(inverse, eye - exact_dot(gram_wide[:, 0:covs], inverse))
     small[1, :, 0:covs] = inverse
-    next_tick()
+    while now() <= min(last, sent_at + far):
+        next_tick()
 
     for k in range(chips):
         block = kept[k]
         fitted = dot(cov_all[k].reshape(2 * rows, LANES), thrice(block[2 * rows :]))
         pheno_all[pl.ds(k * 2 * rows, 2 * rows)] = block[0 : 2 * rows].astype(F32) + fitted
-    next_tick()
     cov_pheno = jnp.zeros((terms, pad), F32)
     for part in split3(pheno_all[...]):
         cov_pheno = cov_pheno + dot(cov_t[0:terms], part)
@@ -392,20 +399,34 @@
     for copy in pair_rows:
         copy.wait_recv()
 
-    def scan(p):
-        dose = dose_all[p].reshape(samples, width)
-        both = dot(lhs[...], dose)
-        cov_dose = (
-            both[genes : genes + covs]
-            + both[genes + covs : genes + 2 * covs]
-            + both[genes + 2 * covs : genes + 3 * covs]
-        )
+    cut = far * 3 // 4 // 4 * 4
+    low, high = cut * 2 * rows, (chips - cut) * 2 * rows
+
+    def part(first, final, p):
+        dose = dose_all[p, first:final].reshape((final - first) * 2 * rows, width)
+        real = dose.astype(F32)
+        return (
+            dot(lhs[:, first * 2 * rows : final * 2 * rows], dose),
+            jnp.sum(real * real, axis=0, keepdims=True),
+        )
+
+    def near_part(p):
+        if cut:
+            before, after = part(0, cut, p), part(chips - cut, chips, p)
+            partial[p] = before[0] + after[0]
+            partial_sq[p, 0:1] = before[1] + after[1]
+        else:
+            partial[p] = jnp.zeros(partial.shape[1:], F32)
+            partial_sq[p] = jnp.zeros(partial_sq.shape[1:], F32)
+
+    def finish(p):
+        both, dose_sq = part(cut, chips - cut, p)
+        both = both + partial[p]
+        dose_sq = dose_sq + partial_sq[p, 0:1]
+        cov_dose = three_rows(both[genes:])
         beta = exact_dot(small[1, :, 0:covs], cov_dose)
         back = exact_dot(small[0, :, 0:covs], beta)
-        real = dose.astype(F32)
-        dose_sumsq = jnp.sum(real * real, axis=0, keepdims=True) - jnp.sum(
-            beta * (2.0 * cov_dose - back), axis=0, keepdims=True
-        )
+        dose_sumsq = dose_sq - jnp.sum(beta * (2.0 * cov_dose - back), axis=0, keepdims=True)
         dose_scale = 1.0 / jnp.sqrt(dose_sumsq / samples + 0.1)
         blank = jnp.zeros((LANES - covs, width), BF16)
         cross = both[0:genes] + dot(
@@ -414,22 +435,28 @@
         scale = gene_scale[...]
         chi_sum, hit_sum = chi_acc[0:genes], hit_acc[0:genes]
         for n in range(width // LANES):
-            cut = slice(n * LANES, (n + 1) * LANES)
-            zscore = cross[:, cut] * dose_scale[:, cut] * scale
+            span = slice(n * LANES, (n + 1) * LANES)
+            zscore = cross[:, span] * dose_scale[:, span] * scale
             chi = zscore * zscore
             chi_sum = chi_sum + chi
             hit_sum = hit_sum + 1.0 / (1.0 + jnp.exp(8.0 - 2.0 * chi))
         chi_acc[0:genes] = chi_sum
         hit_acc[0:genes] = hit_sum
 
-    done = 0
+    def over(work, begin, end):
+        lax.fori_loop(begin, end, lambda p, _: (work(p), 0)[1], 0)
+
+    early = sum(tick_of(p) + far < now() for p in range(PIECES))
+    over(near_part, 0, early)
+    next_tick()
+    over(finish, 0, early)
+    next_tick()
+    while pending and now() <= last - far // 4 + 1:
+        next_tick()
+    over(near_part, early, PIECES)
     while pending:
-        now = pending[0]
-        next_tick()
-        if done < PIECES and tick_of(done) + far < now:
-            scan(done)
-            done += 1
-    lax.fori_loop(done, PIECES, lambda p, _: (scan(p), 0)[1], 0)
+        next_tick()
+    over(finish, early, PIECES)
 
     mine[...] = jnp.zeros_like(mine)
     mine[0:1] = jnp.sum(jnp.transpose(chi_acc[...]), axis=0, keepdims=True)
@@ -440,10 +467,10 @@
         swap(p).wait_send()
         for d in (CW, CCW):
             for step in range(hops(d, p)):
-                ring(d, p, step, source(d, step)).wait_send()
+                ring(d, p, step).wait_send()
     for d in (CW, CCW):
         for step in range(reach[d]):
-            ring_cov(d, step, source(d, step)).wait_send()
+            ring_cov(d, step).wait_send()
             ring_pheno(d, step).wait_send()
     for copy in (pair_tile, pair_raw, pair_cov, *pair_rows):
         copy.wait_send()
@@ -490,6 +517,8 @@
         vmem((genes, LANES), BF16),
         vmem((2, covs, LANES), F32),
         vmem((genes, LANES), F32),
+        vmem((PIECES, genes + 3 * covs, width), F32),
+        vmem((PIECES, 8, width), F32),
         vmem((wide, LANES), F32),
         vmem((wide, LANES), F32),
         vmem((8, wide), F32),

time: 182 us -> 179 us (0.984)
  Pallas kernels: 178 us -> 174 us
    pallas_call x1, Pallas kernels: 178 us -> 174 us  [local(): pl.pallas_call(functools.partial(kernel, chips, genes), out_shape=[jax.Sh...]
where the time goes in v3:
time: 179 us; the launch traced here: 178 us
  Pallas kernels  174 us (97%)
  local copies, waits for them, and re-layouts  3.68 us (2%)
    pallas_call x1, Pallas kernels, local(): pl.pallas_call(functools.partial(kernel, chips, genes), out_shape=[jax.Sh...  174 us
    unnamed x8, local copies, waits for them, and re-layouts  3.68 us

profile of v3, /device:TPU:37, one launch (start us, length us, event | category | flops | bytes accessed | tf_op | source)
XLA Modules:
  0.0 178.3 jit_solution(18192171863538947198)
XLA Ops:
  0.6 0.0 copy-start
  0.6 1.0 copy-done
  1.6 0.0 copy-start.1
  1.7 0.9 copy-done.1
  2.6 0.0 copy-start.2
  2.6 0.7 copy-done.2
  3.3 174.0 %shard_map.50 = (f32[1,112]{1,0:T(1,128)S(1)}, f32[1,112]{1,0:T(1,128)S(1)}) custom-call(bf16[16,8192]{1,0:T(8,128)(2,1)S(1)} %copy-done.1, f32[16,16]{1,0:T(8,128)S(1)} %copy-done.2, f32[16,7168]{1,0:T(8,128)S(1)} %copy-done), custom_call_target="tpu_custom_call" | custom-call | tf_op jit(solution)/shard_map/pallas_call | solution.py:541
  177.3 0.5 copy.7
  177.8 0.5 copy.8
Async XLA Ops:
  0.6 1.0 copy-start
  1.6 0.9 copy-start.1
  2.6 0.7 copy-start.2

commit v4 on v3

--- a/solution.py
+++ b/solution.py
@@ -61,6 +61,9 @@
     gene_scale,
     partial,
     partial_sq,
+    cov_dose_all,
+    dose_sq_all,
+    beta_all,
     chi_acc,
     hit_acc,
     mine,
@@ -115,8 +118,7 @@
     for peer in (partner, right, left):
         pl.semaphore_signal(barrier, inc=1, device_id={"tile": peer}, device_id_type=MESH)
     pl.semaphore_wait(barrier, 3)
-    for copy in loads:
-        copy.wait()
+    loads[0].wait()
 
     def swap(p):
         cols = pl.ds(pl.multiple_of(other * half + p * width, LANES), width)
@@ -195,6 +197,7 @@
 
     launch([p for p in range(PIECES) if tick_of(p) == 0])
 
+    loads[1].wait()
     cov_tile[...] = jnp.zeros_like(cov_tile)
     cov_tile[:, 0:covs] = cov_ref[...]
     hi, mid, lo = split3(cov_tile[...])
@@ -206,6 +209,7 @@
     cov_all[0, c] = packed.astype(BF16)
     chip_tile[c] = packed.astype(BF16)
 
+    loads[2].wait()
     for j in range(chips):
         place = pl.ds(pl.multiple_of(lax.rem(j - z + chips, chips) * pad, LANES), pad)
         for h in range(2):
@@ -320,6 +324,9 @@
                 ring_cov(d, t - 1).wait_recv()
             if 0 < t < reach[d]:
                 ring_cov(d, t).start()
+        for p in sorted(range(PIECES), key=tick_of):
+            if 0 < t - tick_of(p) <= far:
+                forward(p, t - tick_of(p))
         step = t - sent_at
         for d in (CW, CCW):
             if 0 < step <= reach[d]:
@@ -328,9 +335,6 @@
                 ring_pheno(d, step).start()
             if 0 < step <= reach[d]:
                 keep_pheno(d, step - 1)
-        for p in sorted(range(PIECES), key=tick_of):
-            if 0 < t - tick_of(p) <= far:
-                forward(p, t - tick_of(p))
 
     last = max([tick_of(p) for p in range(PIECES)] + [sent_at + 1]) + far
     pending = list(range(1, last + 1))
@@ -419,18 +423,31 @@
             partial[p] = jnp.zeros(partial.shape[1:], F32)
             partial_sq[p] = jnp.zeros(partial_sq.shape[1:], F32)
 
-    def finish(p):
+    def far_part(p):
         both, dose_sq = part(cut, chips - cut, p)
         both = both + partial[p]
-        dose_sq = dose_sq + partial_sq[p, 0:1]
-        cov_dose = three_rows(both[genes:])
+        partial[p, 0:genes] = both[0:genes]
+        place = pl.ds(pl.multiple_of(p * width, LANES), width)
+        cov_dose_all[:, place] = three_rows(both[genes:])
+        dose_sq_all[0:1, place] = dose_sq + partial_sq[p, 0:1]
+
+    def solve_pieces(begin, end):
+        span = slice(begin * width, end * width)
+        cov_dose = cov_dose_all[:, span]
         beta = exact_dot(small[1, :, 0:covs], cov_dose)
         back = exact_dot(small[0, :, 0:covs], beta)
-        dose_sumsq = dose_sq - jnp.sum(beta * (2.0 * cov_dose - back), axis=0, keepdims=True)
-        dose_scale = 1.0 / jnp.sqrt(dose_sumsq / samples + 0.1)
+        dose_sumsq = dose_sq_all[0:1, span] - jnp.sum(
+            beta * (2.0 * cov_dose - back), axis=0, keepdims=True
+        )
+        dose_sq_all[0:1, span] = 1.0 / jnp.sqrt(dose_sumsq / samples + 0.1)
+        beta_all[:, span] = beta.astype(BF16)
+
+    def score(p):
+        place = pl.ds(pl.multiple_of(p * width, LANES), width)
+        dose_scale = dose_sq_all[0:1, place]
         blank = jnp.zeros((LANES - covs, width), BF16)
-        cross = both[0:genes] + dot(
-            lhs_fix[...], jnp.concatenate([beta.astype(BF16), blank], axis=0)
+        cross = partial[p, 0:genes] + dot(
+            lhs_fix[...], jnp.concatenate([beta_all[:, place], blank], axis=0)
         )
         scale = gene_scale[...]
         chi_sum, hit_sum = chi_acc[0:genes], hit_acc[0:genes]
@@ -443,20 +460,26 @@
         chi_acc[0:genes] = chi_sum
         hit_acc[0:genes] = hit_sum
 
+    def finish(begin, end):
+        over(far_part, begin, end)
+        if end > begin:
+            solve_pieces(begin, end)
+        over(score, begin, end)
+
     def over(work, begin, end):
         lax.fori_loop(begin, end, lambda p, _: (work(p), 0)[1], 0)
 
     early = sum(tick_of(p) + far < now() for p in range(PIECES))
     over(near_part, 0, early)
     next_tick()
-    over(finish, 0, early)
+    finish(0, early)
     next_tick()
     while pending and now() <= last - far // 4 + 1:
         next_tick()
     over(near_part, early, PIECES)
     while pending:
         next_tick()
-    over(finish, early, PIECES)
+    finish(early, PIECES)
 
     mine[...] = jnp.zeros_like(mine)
     mine[0:1] = jnp.sum(jnp.transpose(chi_acc[...]), axis=0, keepdims=True)
@@ -519,6 +542,9 @@
         vmem((genes, LANES), F32),
         vmem((PIECES, genes + 3 * covs, width), F32),
         vmem((PIECES, 8, width), F32),
+        vmem((covs, PIECES * width), F32),
+        vmem((8, PIECES * width), F32),
+        vmem((covs, PIECES * width), BF16),
         vmem((wide, LANES), F32),
         vmem((wide, LANES), F32),
         vmem((8, wide), F32),

time: 179 us -> 176 us (0.983)
  Pallas kernels: 174 us -> 171 us
    pallas_call x1, Pallas kernels: 174 us -> 171 us  [local(): pl.pallas_call(functools.partial(kernel, chips, genes), out_shape=[jax.Sh...]
where the time goes in v4:
time: 176 us; the launch traced here: 175 us
  Pallas kernels  171 us (97%)
  local copies, waits for them, and re-layouts  3.68 us (2%)
    pallas_call x1, Pallas kernels, local(): pl.pallas_call(functools.partial(kernel, chips, genes), out_shape=[jax.Sh...  171 us
    unnamed x8, local copies, waits for them, and re-layouts  3.68 us

profile of v4, /device:TPU:37, one launch (start us, length us, event | category | flops | bytes accessed | tf_op | source)
XLA Modules:
  0.0 175.4 jit_solution(10626869400669844945)
XLA Ops:
  0.6 0.0 copy-start
  0.6 1.0 copy-done
  1.6 0.0 copy-start.1
  1.7 0.9 copy-done.1
  2.6 0.0 copy-start.2
  2.6 0.7 copy-done.2
  3.3 171.1 %shard_map.50 = (f32[1,112]{1,0:T(1,128)S(1)}, f32[1,112]{1,0:T(1,128)S(1)}) custom-call(bf16[16,8192]{1,0:T(8,128)(2,1)S(1)} %copy-done.1, f32[16,16]{1,0:T(8,128)S(1)} %copy-done.2, f32[16,7168]{1,0:T(8,128)S(1)} %copy-done), custom_call_target="tpu_custom_call" | custom-call | tf_op jit(solution)/shard_map/pallas_call | solution.py:567
  174.4 0.5 copy.7
  174.9 0.5 copy.8
Async XLA Ops:
  0.6 1.0 copy-start
  1.6 0.9 copy-start.1
  2.6 0.7 copy-start.2

commit v5 on v4

--- a/solution.py
+++ b/solution.py
@@ -317,7 +317,7 @@
 
     sent_at = 2 + PHENO_TICK
 
-    def tick(t):
+    def tick(t, then=None):
         launch([p for p in range(PIECES) if t > 0 and tick_of(p) == t])
         for d in (CW, CCW):
             if 0 < t <= reach[d]:
@@ -327,6 +327,8 @@
         for p in sorted(range(PIECES), key=tick_of):
             if 0 < t - tick_of(p) <= far:
                 forward(p, t - tick_of(p))
+                if then and t - tick_of(p) == far:
+                    then(p)
         step = t - sent_at
         for d in (CW, CCW):
             if 0 < step <= reach[d]:
@@ -342,9 +344,9 @@
     def now():
         return pending[0] if pending else last + 1
 
-    def next_tick():
+    def next_tick(then=None):
         if pending:
-            tick(pending.pop(0))
+            tick(pending.pop(0), then)
 
     for _ in range(sent_at - 2):
         next_tick()
@@ -461,7 +463,6 @@
         hit_acc[0:genes] = hit_sum
 
     def finish(begin, end):
-        over(far_part, begin, end)
         if end > begin:
             solve_pieces(begin, end)
         over(score, begin, end)
@@ -472,13 +473,24 @@
     early = sum(tick_of(p) + far < now() for p in range(PIECES))
     over(near_part, 0, early)
     next_tick()
+    over(far_part, 0, early)
     finish(0, early)
     next_tick()
     while pending and now() <= last - far // 4 + 1:
         next_tick()
     over(near_part, early, PIECES)
+    landed = []
+
+    def land(p):
+        if p >= early:
+            far_part(p)
+            landed.append(p)
+
     while pending:
-        next_tick()
+        next_tick(land)
+    for p in range(early, PIECES):
+        if p not in landed:
+            far_part(p)
     finish(early, PIECES)
 
     mine[...] = jnp.zeros_like(mine)

time: 176 us -> 175 us (level)
  no operation moved by 1% of the time
where the time goes in v5:
time: 175 us; the launch traced here: 174 us
  Pallas kernels  170 us (97%)
  local copies, waits for them, and re-layouts  3.68 us (2%)
    pallas_call x1, Pallas kernels, local(): pl.pallas_call(functools.partial(kernel, chips, genes), out_shape=[jax.Sh...  170 us
    unnamed x8, local copies, waits for them, and re-layouts  3.68 us

profile of v5, /device:TPU:37, one launch (start us, length us, event | category | flops | bytes accessed | tf_op | source)
XLA Modules:
  0.0 174.3 jit_solution(5730274590892699366)
XLA Ops:
  0.6 0.0 copy-start
  0.6 1.0 copy-done
  1.6 0.0 copy-start.1
  1.7 0.9 copy-done.1
  2.6 0.0 copy-start.2
  2.6 0.7 copy-done.2
  3.3 170.0 %shard_map.50 = (f32[1,112]{1,0:T(1,128)S(1)}, f32[1,112]{1,0:T(1,128)S(1)}) custom-call(bf16[16,8192]{1,0:T(8,128)(2,1)S(1)} %copy-done.1, f32[16,16]{1,0:T(8,128)S(1)} %copy-done.2, f32[16,7168]{1,0:T(8,128)S(1)} %copy-done), custom_call_target="tpu_custom_call" | custom-call | tf_op jit(solution)/shard_map/pallas_call | solution.py:579
  173.3 0.5 copy.7
  173.8 0.5 copy.8
Async XLA Ops:
  0.6 1.0 copy-start
  1.6 0.9 copy-start.1
  2.6 0.7 copy-start.2

commit v6 on v5

--- a/solution.py
+++ b/solution.py
@@ -327,8 +327,8 @@
         for p in sorted(range(PIECES), key=tick_of):
             if 0 < t - tick_of(p) <= far:
                 forward(p, t - tick_of(p))
-                if then and t - tick_of(p) == far:
-                    then(p)
+                if then:
+                    then(p, t - tick_of(p))
         step = t - sent_at
         for d in (CW, CCW):
             if 0 < step <= reach[d]:
@@ -478,11 +478,21 @@
     next_tick()
     while pending and now() <= last - far // 4 + 1:
         next_tick()
-    over(near_part, early, PIECES)
+    ready = []
+
+    def prepare(p, step):
+        if p >= early and step > cut and p not in ready:
+            near_part(p)
+            ready.append(p)
+
+    next_tick(prepare)
+    for p in range(early, PIECES):
+        if p not in ready:
+            near_part(p)
     landed = []
 
-    def land(p):
-        if p >= early:
+    def land(p, step):
+        if p >= early and step == far:
             far_part(p)
             landed.append(p)
 

time: 175 us -> 174 us (level)
  no operation moved by 1% of the time
where the time goes in v6:
time: 174 us
  Pallas kernels  170 us (98%)
  local copies, waits for them, and re-layouts  3.68 us (2%)
    pallas_call x1, Pallas kernels, local(): pl.pallas_call(functools.partial(kernel, chips, genes), out_shape=[jax.Sh...  170 us
    unnamed x8, local copies, waits for them, and re-layouts  3.68 us

profile of v6, /device:TPU:37, one launch (start us, length us, event | category | flops | bytes accessed | tf_op | source)
XLA Modules:
  0.0 174.0 jit_solution(12756915985064325566)
XLA Ops:
  0.6 0.0 copy-start
  0.6 1.0 copy-done
  1.6 0.0 copy-start.1
  1.7 0.9 copy-done.1
  2.6 0.0 copy-start.2
  2.6 0.7 copy-done.2
  3.3 169.7 %shard_map.50 = (f32[1,112]{1,0:T(1,128)S(1)}, f32[1,112]{1,0:T(1,128)S(1)}) custom-call(bf16[16,8192]{1,0:T(8,128)(2,1)S(1)} %copy-done.1, f32[16,16]{1,0:T(8,128)S(1)} %copy-done.2, f32[16,7168]{1,0:T(8,128)S(1)} %copy-done), custom_call_target="tpu_custom_call" | custom-call | tf_op jit(solution)/shard_map/pallas_call | solution.py:589
  173.0 0.5 copy.7
  173.5 0.5 copy.8
Async XLA Ops:
  0.6 1.0 copy-start
  1.6 0.9 copy-start.1
  2.6 0.7 copy-start.2
